TPU v7x, 16 devices: a whole 2x2x2 slice. The times are simulated.
16 devices in a mesh: ep: 16 (over z, y, x, core).
Axes of the slice: x: 2, y: 2, z: 2, core: 2. Of those that a mesh axis runs over, the one named last changes fastest.
Arguments:
- hidden: bfloat16 [2048, 4096], P('ep')
- grad_out: bfloat16 [2048, 4096], P('ep')
- w_router: bfloat16 [4096, 16], replicated
- b_router: float32 [16], replicated
- expert_ids: int32 [2048, 4], P('ep')
- slot_ids: int32 [2048, 4], P('ep')
- w_gate_up: bfloat16 [16, 4096, 1376], P('ep')
- b_gate_up: float32 [16, 1376], P('ep')
- w_down: bfloat16 [16, 688, 4096], P('ep')
- b_down: float32 [16, 4096], P('ep')
Outputs:
- output 1: bfloat16 [2048, 4096], P('ep')
- output 2: bfloat16 [2048, 4096], P('ep')
- output 3: float32 [4096, 16], replicated
- output 4: float32 [16], replicated
- output 5: float32 [16, 4096, 1376], P('ep')
- output 6: float32 [16, 1376], P('ep')
- output 7: float32 [16, 688, 4096], P('ep')
- output 8: float32 [16, 4096], P('ep')
All inputs are finite; a program needn't handle non-finite values.
Results may differ from a plain program's by a relative error of at most 0.0100469.
Values are sent between devices in bfloat16 or wider.
A program may use at most 1 GiB of HBM per device.

v0:
```python
import jax
import jax.numpy as jnp
from jax import lax
from jax.sharding import PartitionSpec as P

SWIGLU_LIMIT = 7.0
SWIGLU_ALPHA = 1.702


def swiglu(pre_act):
    col_pairs = pre_act.reshape(pre_act.shape[:-1] + (pre_act.shape[-1] // 2, 2))
    gate_in = jnp.minimum(col_pairs[..., 0], SWIGLU_LIMIT)
    up_in = jnp.clip(col_pairs[..., 1], -SWIGLU_LIMIT, SWIGLU_LIMIT)
    return gate_in * jax.nn.sigmoid(SWIGLU_ALPHA * gate_in) * (up_in + 1.0)


def solution(mesh):
    ep_size = mesh.shape['ep']

    def local_block(hidden, grad_out, w_router, b_router, expert_ids, slot_ids, w_gate_up, b_gate_up, w_down, b_down):
        tok_local, d_model = hidden.shape
        top_k = expert_ids.shape[1]
        experts = w_router.shape[1]
        local_experts = w_gate_up.shape[0]
        capacity = (3 * tok_local * top_k + 2 * experts - 1) // (2 * experts)
        buf_rows = experts * capacity
        copy_count = tok_local * top_k
        dest_row = jnp.where(slot_ids >= 0, expert_ids * capacity + slot_ids, buf_rows)
        src_copy = jnp.full((buf_rows + 1,), copy_count, jnp.int32).at[dest_row.reshape(-1)].set(jnp.arange(copy_count, dtype=jnp.int32))[:buf_rows]
        src_tok = src_copy // top_k
        logits = jnp.dot(hidden, w_router, preferred_element_type=jnp.float32) + b_router
        gate_w = jax.nn.softmax(jnp.take_along_axis(logits, expert_ids, axis=1), axis=-1)

        send_x = jnp.take(hidden, src_tok, axis=0, mode='fill', fill_value=0)
        recv_x = lax.all_to_all(send_x, 'ep', 0, 0, tiled=True).reshape(ep_size, local_experts, capacity, d_model)
        pre_act = jnp.einsum('secd,edf->secf', recv_x, w_gate_up, preferred_element_type=jnp.float32) + b_gate_up[None, :, None, :]
        act_val, act_vjp = jax.vjp(swiglu, pre_act)
        act_bf = act_val.astype(jnp.bfloat16)
        y_rows = (jnp.einsum('secf,efd->secd', act_bf, w_down, preferred_element_type=jnp.float32) + b_down[None, :, None, :]).astype(jnp.bfloat16)
        back_y = lax.all_to_all(y_rows.reshape(buf_rows, d_model), 'ep', 0, 0, tiled=True)
        y_copies = jnp.take(back_y, dest_row, axis=0, mode='fill', fill_value=0)
        block_out = jnp.sum(gate_w[:, :, None] * y_copies, axis=1).astype(jnp.bfloat16)

        gate_grad = jnp.einsum('td,tkd->tk', grad_out, y_copies, preferred_element_type=jnp.float32)
        sel_grad = gate_w * (gate_grad - jnp.sum(gate_w * gate_grad, axis=1, keepdims=True))
        expert_range = jnp.arange(experts, dtype=jnp.int32)
        logit_grad = jnp.sum(jnp.where(expert_ids[:, :, None] == expert_range, sel_grad[:, :, None], 0.0), axis=1).astype(jnp.bfloat16)
        row_gate = jnp.take(gate_w.reshape(-1), src_copy, axis=0, mode='fill', fill_value=0)
        row_grad = jnp.take(grad_out, src_tok, axis=0, mode='fill', fill_value=0)
        send_q = (row_gate[:, None] * row_grad).astype(jnp.bfloat16)
        recv_q = lax.all_to_all(send_q, 'ep', 0, 0, tiled=True).reshape(ep_size, local_experts, capacity, d_model)
        grad_b_down = jnp.sum(recv_q, axis=(0, 2), dtype=jnp.float32)
        grad_w_down = jnp.einsum('secf,secd->efd', act_bf, recv_q, preferred_element_type=jnp.float32)
        act_grad = jnp.einsum('secd,efd->secf', recv_q, w_down, preferred_element_type=jnp.float32)
        pre_grad = act_vjp(act_grad)[0].astype(jnp.bfloat16)
        grad_b_gate_up = jnp.sum(pre_grad, axis=(0, 2), dtype=jnp.float32)
        grad_w_gate_up = jnp.einsum('secd,secf->edf', recv_x, pre_grad, preferred_element_type=jnp.float32)
        p_rows = jnp.einsum('secf,edf->secd', pre_grad, w_gate_up, preferred_element_type=jnp.float32).astype(jnp.bfloat16)
        back_p = lax.all_to_all(p_rows.reshape(buf_rows, d_model), 'ep', 0, 0, tiled=True)
        p_copies = jnp.take(back_p, dest_row, axis=0, mode='fill', fill_value=0)
        router_dx = jnp.einsum('te,de->td', logit_grad, w_router, preferred_element_type=jnp.float32)
        grad_hidden = (jnp.sum(p_copies, axis=1, dtype=jnp.float32) + router_dx).astype(jnp.bfloat16)
        grad_w_router = lax.psum(jnp.einsum('td,te->de', hidden, logit_grad, preferred_element_type=jnp.float32), 'ep')
        grad_b_router = lax.psum(jnp.sum(logit_grad, axis=0, dtype=jnp.float32), 'ep')
        return (block_out, grad_hidden, grad_w_router, grad_b_router, grad_w_gate_up, grad_b_gate_up, grad_w_down, grad_b_down)

    tok_spec = P('ep', None)
    in_specs = (tok_spec, tok_spec, P(None, None), P(None), tok_spec, tok_spec, P('ep', None, None), P('ep', None), P('ep', None, None), P('ep', None))
    out_specs = (tok_spec, tok_spec, P(None, None), P(None), P('ep', None, None), P('ep', None), P('ep', None, None), P('ep', None))
    return jax.shard_map(local_block, mesh=mesh, in_specs=in_specs, out_specs=out_specs, check_vma=False)
```

profile of v0, /device:TPU:0, one launch (start us, length us, event | category | flops | bytes accessed | tf_op | source)
XLA Modules:
  0.0 623.9 jit_solution(18223479331223290663)
XLA Ops:
  7.2 0.8 compare_and_fusion.1
  8.0 0.1 copy.82
  8.2 2.4 scatter_custom_fusion
  10.7 13.3 %gather_fusion.2 = bf16[768,4096]{1,0:T(8,128)(2,1)} fusion(bf16[128,4096]{1,0:T(8,128)(2,1)} %param.14, s32[1024]{0:T(1024)S(1)} %pad_clamp_fusion.2), kind=kCustom, calls=%fused_computation.clone | custom fusion | bytes 12585984 | tf_op jit(solution)/shard_map/jit(_take)/gather | solution.py:34
  24.0 6.0 broadcast_select_fusion
  30.0 5.6 all-to-all-start
  35.6 80.4 %all-to-all-done = bf16[16,48,4096]{2,1,0:T(8,128)(2,1)} async-done(((bf16[16,48,4096]{2,1,0:T(8,128)(2,1)}), bf16[16,48,4096]{2,1,0:T(8,128)(2,1)}, u32[]{:S(2)}, u32[]{:S(2)}) %all-to-all-start) | async-done | bytes 6291488 | tf_op jit(solution)/shard_map/all_to_all | solution.py:35
  116.0 16.0 %fusion.13 = f32[16,1,48,1376]{3,2,0,1:T(8,128)} fusion(bf16[16,48,4096]{2,1,0:T(8,128)(2,1)} %all-to-all-done, bf16[1,4096,1376]{1,2,0:T(8,128)(2,1)} %param.20, f32[1376]{0:T(1024)S(1)} %reduce.5), kind=kOutput, calls=%fused_computation.31 | convolution fusion | flops 8658100224 | bytes 21796224 | tf_op jit(solution)/shard_map/secd,edf->secf/dot_general | solution.py:36
  132.0 10.1 %copy.83 = f32[16,1,48,1376]{2,0,3,1:T(8,128)} copy(f32[16,1,48,1376]{3,2,0,1:T(8,128)} %fusion.13) | data formatting | bytes 8454144 | tf_op jit(solution)/shard_map/add | solution.py:36
  142.1 9.4 %fusion.67 = (f32[16,1,48,688,1]{2,0,4,3,1:T(8,128)}, f32[16,1,48,688,1]{2,0,4,3,1:T(8,128)}) fusion(f32[16,1,48,688,2]{2,0,4,3,1:T(8,128)} %bitcast.154), kind=kLoop, calls=%fused_computation.119 | loop fusion | bytes 8454144 | tf_op jit(solution)/shard_map/jvp()/slice | solution.py:13
  151.5 4.9 copy.97
  156.3 6.9 %copy.96 = f32[16,1,48,688,1]{3,2,0,4,1:T(8,128)} copy(f32[16,1,48,688,1]{2,0,4,3,1:T(8,128)} %get-tuple-element.23) | data formatting | bytes 4227072
  163.3 10.1 %fusion.8 = bf16[16,48,4096]{2,1,0:T(8,128)(2,1)} fusion(f32[4096]{0:T(1024)S(1)} %bitcast.160, bf16[1,688,4096]{2,1,0:T(8,128)(2,1)} %param.22, f32[16,1,48,688,1]{3,2,0,4,1:T(8,128)} %copy.96, f32[16,1,48,688,1]{3,2,0,4,1:T(8,128)S(1)} %copy.97), kind=kOutput, calls=%fused_computation.21 | convolution fusion | flops 4340097024 | bytes 16171008 | tf_op jit(solution)/shard_map/secf,efd->secd/dot_general | solution.py:39
  173.4 4.9 all-to-all-start.1
  178.4 0.1 copy.81
  178.5 0.1 copy.86
  178.8 0.1 copy.78
  179.0 0.4 convolution_add_fusion.1
  179.4 3.8 gather_fusion.1
  183.3 5.7 gather_fusion.4
  189.1 69.7 %all-to-all-done.1 = bf16[16,48,4096]{2,1,0:T(8,128)(2,1)} async-done(((bf16[16,48,4096]{2,1,0:T(8,128)(2,1)}), bf16[16,48,4096]{2,1,0:T(8,128)(2,1)}, u32[]{:S(2)}, u32[]{:S(2)}) %all-to-all-start.1) | async-done | bytes 6291488 | tf_op jit(solution)/shard_map/all_to_all | solution.py:40
  258.8 12.2 %gather_fusion.3 = bf16[512,4096]{1,0:T(8,128)(2,1)} fusion(bf16[768,4096]{1,0:T(8,128)(2,1)} %bitcast.17, s32[1024]{0:T(1024)S(1)} %pad_clamp_fusion.1), kind=kCustom, calls=%fused_computation.1.clone | custom fusion | bytes 8390656 | tf_op jit(solution)/shard_map/jit(_take)/gather | solution.py:41
  271.0 7.2 %reshape.472 = bf16[128,4,4096]{2,1,0:T(4,128)(2,1)} reshape(bf16[512,4096]{1,0:T(8,128)(2,1)} %gather_fusion.3) | data formatting | bytes 8388608 | tf_op jit(solution)/shard_map/jit(_take)/gather | solution.py:41
  278.2 8.4 %fusion.16 = f32[128,1,4]{2,1,0:T(1,128)S(1)} fusion(bf16[128,4,4096]{2,1,0:T(4,128)(2,1)} %reshape.472, pred[128,4]{1,0:T(8,128)(4,1)S(1)} %copy.81, bf16[128,4096,1]{1,0,2:T(8,128)(2,1)S(1)} %bitcast.153), kind=kOutput, calls=%fused_computation.34 | convolution fusion | flops 6291456 | bytes 5245440 | tf_op jit(solution)/shard_map/td,tkd->tk/dot_general | solution.py:44
  286.7 0.1 copy.80
  286.9 5.2 gather_fusion
  292.1 9.5 %multiply_convert_fusion = bf16[768,4096]{1,0:T(8,128)(2,1)} fusion(bf16[768,4096]{1,0:T(8,128)(2,1)} %gather_fusion.4, f32[768]{0:T(1024)S(1)} %and_select_fusion, pred[768]{0:T(1024)(128)(4,1)S(1)} %get-tuple-element.18), kind=kLoop, calls=%fused_computation.11 | loop fusion | flops 12582912 | bytes 12586752 | tf_op jit(solution)/shard_map/convert_element_type | solution.py:50
  301.7 4.5 all-to-all-start.2
  306.2 80.4 %all-to-all-done.2 = bf16[16,48,4096]{2,1,0:T(8,128)(2,1)} async-done(((bf16[16,48,4096]{2,1,0:T(8,128)(2,1)}), bf16[16,48,4096]{2,1,0:T(8,128)(2,1)}, u32[]{:S(2)}, u32[]{:S(2)}) %all-to-all-start.2) | async-done | bytes 6291488 | tf_op jit(solution)/shard_map/all_to_all | solution.py:51
  386.7 11.9 %fusion.29 = (f32[16,1,48,688,1]{3,2,0,4,1:T(8,128)S(1)}, f32[16,1,48,688,1]{3,2,0,4,1:T(8,128)S(1)}) fusion(f32[16,1,48,688,1]{3,2,0,4,1:T(8,128)} %copy-done.3, f32[16,1,48,688,1]{3,2,0,4,1:T(8,128)} %copy.96, bf16[16,48,4096]{2,1,0:T(8,128)(2,1)} %all-to-all-done.2, bf16[1,688,4096]{2,1,0:T(8,128)(2,1)} %param.22), kind=kOutput, calls=%fused_computation.52 | convolution fusion | flops 4345958400 | bytes 20381696 | tf_op jit(solution)/shard_map/secd,efd->secf/dot_general | solution.py:54
  398.6 1.9 convert_reduce_fusion.2
  400.4 9.6 %copy.89 = bf16[16,1,48,688,2]{2,0,4,3,1:T(8,128)(2,1)} copy(bf16[16,1,48,688,2]{3,2,0,4,1:T(8,128)(2,1)} %get-tuple-element.13) | data formatting | bytes 4227072 | tf_op jit(solution)/shard_map/convert_element_type | solution.py:55
  410.1 7.3 %copy.90 = bf16[16,48,1376]{2,1,0:T(8,128)(2,1)} copy(bf16[16,48,1376]{1,0,2:T(8,128)(2,1)} %bitcast.157) | data formatting | bytes 4227072 | tf_op jit(solution)/shard_map/convert_element_type | solution.py:55
  417.4 15.0 %fusion.5 = bf16[16,48,4096]{2,1,0:T(8,128)(2,1)} fusion(bf16[16,48,1376]{2,1,0:T(8,128)(2,1)} %copy.90, bf16[1,4096,1376]{1,2,0:T(8,128)(2,1)} %param.20), kind=kOutput, calls=%fused_computation.19 | convolution fusion | flops 8660189184 | bytes 19677184 | tf_op jit(solution)/shard_map/secf,edf->secd/dot_general | solution.py:58
  432.4 4.5 all-to-all-start.3
  437.0 0.1 convert_reduce_fusion.3
  437.1 107.3 %psum.15 = f32[16]{0:T(128)} all-reduce(f32[16]{0:T(128)S(1)} %convert_reduce_fusion.3), channel_id=1, replica_groups=mesh['ep'=16] {'ep'}, use_global_device_ids=true, to_apply=%region_9.12 | all-reduce | flops 16 | bytes 128 | tf_op jit(solution)/shard_map/psum | solution.py:64
  544.4 1.0 convolution_bitcast_fusion.2
  545.3 0.2 copy.93
  545.5 0.8 reduce_sum.83
  546.4 4.5 convert_reduce_fusion
  550.8 16.3 %convolution_bitcast_fusion = f32[1,4096,1376]{1,2,0:T(8,128)} fusion(bf16[16,48,4096]{2,1,0:T(8,128)(2,1)} %all-to-all-done, bf16[16,48,1376]{2,1,0:T(8,128)(2,1)} %copy.90), kind=kOutput, calls=%fused_computation.7 | convolution fusion | flops 8657043456 | bytes 30949376 | tf_op jit(solution)/shard_map/secd,secf->edf/dot_general | solution.py:57
  567.1 10.8 %convolution_bitcast_fusion.1 = f32[1,688,4096]{2,1,0:T(8,128)} fusion(bf16[16,48,4096]{2,1,0:T(8,128)(2,1)} %all-to-all-done.2, f32[16,1,48,688,1]{3,2,0,4,1:T(8,128)S(1)} %copy-done.5, f32[16,1,48,688,1]{3,2,0,4,1:T(8,128)S(1)} %copy-done.4), kind=kOutput, calls=%fused_computation.18 | convolution fusion | flops 4333805568 | bytes 21790720 | tf_op jit(solution)/shard_map/secf,secd->efd/dot_general | solution.py:53
  577.9 12.4 %gather_fusion.5 = bf16[512,4096]{1,0:T(8,128)(2,1)} fusion(bf16[768,4096]{1,0:T(8,128)(2,1)} %bitcast.32, s32[1024]{0:T(1024)S(1)} %pad_clamp_fusion.1), kind=kCustom, calls=%fused_computation.3.clone | custom fusion | bytes 8390656 | tf_op jit(solution)/shard_map/jit(_take)/gather | solution.py:60
  590.3 7.2 %reshape.478 = bf16[128,4,4096]{2,1,0:T(4,128)(2,1)} reshape(bf16[512,4096]{1,0:T(8,128)(2,1)} %gather_fusion.5) | data formatting | bytes 8388608 | tf_op jit(solution)/shard_map/jit(_take)/gather | solution.py:60
  597.5 16.0 %convert_reduce_fusion.1 = (f32[128,4096]{1,0:T(8,128)S(1)}, bf16[128,4096]{1,0:T(8,128)(2,1)}) fusion(bf16[128,4,4096]{2,1,0:T(4,128)(2,1)} %reshape.478, pred[128,4]{1,0:T(8,128)(4,1)S(1)} %copy.81, bf16[128,4,4096]{2,1,0:T(4,128)(2,1)} %reshape.472, f32[128,4]{1,0:T(8,128)S(1)} %copy.80), kind=kLoop, calls=%fused_computation.16 | loop fusion | flops 13631488 | bytes 11536896 | tf_op jit(solution)/shard_map/reduce_sum | solution.py:62
  613.5 1.4 fusion.12
  615.0 1.7 copy.101
  (49 shorter events, 1.0 us)
Async XLA Ops:
  7.2 176.2 %copy-start = (bf16[128,4096]{1,0:T(8,128)(2,1)S(1)}, bf16[128,4096]{1,0:T(8,128)(2,1)}, u32[]{:S(2)}) copy-start(bf16[128,4096]{1,0:T(8,128)(2,1)} %param.15) | copy-start | bytes 3145732
  30.0 5.6 copy-start.8
  30.0 86.0 %all-to-all-start = ((bf16[16,48,4096]{2,1,0:T(8,128)(2,1)}), bf16[16,48,4096]{2,1,0:T(8,128)(2,1)}, u32[]{:S(2)}, u32[]{:S(2)}) async-start(bf16[16,48,4096]{2,1,0:T(8,128)(2,1)} %bitcast.156), calls=%async_computation | async-start | bytes 12582912 | tf_op jit(solution)/shard_map/all_to_all | solution.py:35
  156.3 6.9 %copy-start.3 = (f32[16,1,48,688,1]{3,2,0,4,1:T(8,128)}, f32[16,1,48,688,1]{3,2,0,4,1:T(8,128)S(1)}, u32[]{:S(2)}) copy-start(f32[16,1,48,688,1]{3,2,0,4,1:T(8,128)S(1)} %copy.97) | copy-start | bytes 6340612
  156.3 6.9 %copy-start.10 = (f32[1,4096]{1,0:T(1,128)S(1)}, f32[1,4096]{1,0:T(1,128)}, u32[]{:S(2)}) copy-start(f32[1,4096]{1,0:T(1,128)} %param.23) | copy-start | bytes 49156
  173.4 5.3 copy-start.7
  173.4 5.6 copy-start.2
  173.4 5.6 copy-start.6
  173.4 5.6 copy-start.9
  173.4 85.4 %all-to-all-start.1 = ((bf16[16,48,4096]{2,1,0:T(8,128)(2,1)}), bf16[16,48,4096]{2,1,0:T(8,128)(2,1)}, u32[]{:S(2)}, u32[]{:S(2)}) async-start(bf16[16,48,4096]{2,1,0:T(8,128)(2,1)} %fusion.8), calls=%async_computation.1 | async-start | bytes 12582912 | tf_op jit(solution)/shard_map/all_to_all | solution.py:40
  301.7 85.0 %all-to-all-start.2 = ((bf16[16,48,4096]{2,1,0:T(8,128)(2,1)}), bf16[16,48,4096]{2,1,0:T(8,128)(2,1)}, u32[]{:S(2)}, u32[]{:S(2)}) async-start(bf16[16,48,4096]{2,1,0:T(8,128)(2,1)} %bitcast.155), calls=%async_computation.2 | async-start | bytes 12582912 | tf_op jit(solution)/shard_map/all_to_all | solution.py:51
  432.4 145.5 %all-to-all-start.3 = ((bf16[16,48,4096]{2,1,0:T(8,128)(2,1)}), bf16[16,48,4096]{2,1,0:T(8,128)(2,1)}, u32[]{:S(2)}, u32[]{:S(2)}) async-start(bf16[16,48,4096]{2,1,0:T(8,128)(2,1)} %fusion.5), calls=%async_computation.3 | async-start | bytes 12582912 | tf_op jit(solution)/shard_map/all_to_all | solution.py:59
  436.9 178.1 %all-reduce.4.cloned.1.call-start = ((), (), s32[]{:S(2)}) async-start(), calls=%async_computation.4 | async-start | bytes 524288 | tf_op jit(solution)/shard_map/psum | solution.py:63
  550.8 16.3 %copy-start.4 = (f32[16,1,48,688,1]{3,2,0,4,1:T(8,128)S(1)}, f32[16,1,48,688,1]{3,2,0,4,1:T(8,128)}, u32[]{:S(2)}) copy-start(f32[16,1,48,688,1]{3,2,0,4,1:T(8,128)} %copy-done.3) | copy-start | bytes 6340612
  550.8 16.3 %copy-start.5 = (f32[16,1,48,688,1]{3,2,0,4,1:T(8,128)S(1)}, f32[16,1,48,688,1]{3,2,0,4,1:T(8,128)}, u32[]{:S(2)}) copy-start(f32[16,1,48,688,1]{3,2,0,4,1:T(8,128)} %copy.96) | copy-start | bytes 6340612
  597.5 19.1 %copy-start.1 = (bf16[128,4096]{1,0:T(8,128)(2,1)S(1)}, bf16[128,4096]{1,0:T(8,128)(2,1)}, u32[]{:S(2)}) copy-start(bf16[128,4096]{1,0:T(8,128)(2,1)} %param.15) | copy-start | bytes 3145732
Sparse Core Ops, SparseCore 0:
  545.5 66.6 all-reduce.3
where the time goes:
time: 630 us; the launch traced here: 624 us
  waiting for transfers between devices  231 us (37%)
  local copies, waits for them, and re-layouts  122 us (19%)
  blocking collectives  107 us (17%)
  matrix products  91.2 us (14%)
  other arithmetic  39 us (6%)
  starting transfers between devices  19.6 us (3%)
  between operations  14.7 us (2%)
    psum x1, blocking collectives, local_block(): lax.psum(jnp.sum(logit_grad, axis=0, dtype=jnp.float32), 'ep')  107 us
    all_to_all x1, waiting for transfers between devices, local_block(): lax.all_to_all(send_q, 'ep', 0, 0, tiled=True)  80.4 us
    all_to_all x1, waiting for transfers between devices, local_block(): lax.all_to_all(send_x, 'ep', 0, 0, tiled=True)  80.4 us
    all_to_all x1, waiting for transfers between devices, local_block(): lax.all_to_all(y_rows.reshape(buf_rows, d_model), 'ep', 0, 0, tiled=True)  69.7 us
    gather x2, local copies, waits for them, and re-layouts, local_block(): p_copies = jnp.take(back_p, dest_row, axis=0, mode='fill', fill_value=0)  19.6 us
    gather x2, local copies, waits for them, and re-layouts, local_block(): y_copies = jnp.take(back_y, dest_row, axis=0, mode='fill', fill_value=0)  19.4 us
    convert_element_type x2, local copies, waits for them, and re-layouts, local_block(): pre_grad = act_vjp(act_grad)[0].astype(jnp.bfloat16)  16.9 us
    dot_general x1, matrix products, local_block(): jnp.einsum('secd,secf->edf', recv_x, pre_grad, preferred_element_type=jnp...  16.3 us
  transfers between devices with their start and end apart: 5, of which 3 were waited for; matrix products, arithmetic and copies ran while one was open for 13% of the time, Pallas kernels for 0%

commit v1 on v0

v1 whole, which is shorter than its diff:
```python
import functools

import jax
import jax.numpy as jnp
from jax import lax
from jax.experimental import pallas as pl
from jax.experimental.pallas import tpu as pltpu
from jax.sharding import PartitionSpec as P

SWIGLU_LIMIT = 7.0
SWIGLU_ALPHA = 1.702
MESH_ID = pl.DeviceIdType.MESH
BF = jnp.bfloat16
F32 = jnp.float32

DIMS = (2, 4, 8)
CHIP_ORDER = (3, 4, 5, 2, 6, 1, 7)
NDEV = 16


def flip(me, mask):
    out = 0
    for b in (1, 2, 4, 8):
        bit = lax.rem(lax.div(me, b), 2)
        if isinstance(mask, int):
            if mask & b:
                bit = 1 - bit
        else:
            bit = lax.rem(bit + lax.rem(lax.div(mask, b), 2), 2)
        out = out + b * bit
    return out


def split3(v):
    hi = v.astype(BF)
    rest = v - hi.astype(F32)
    mid = rest.astype(BF)
    low = (rest - mid.astype(F32)).astype(BF)
    return hi, mid, low


def dot(a, b):
    return jnp.dot(a, b, preferred_element_type=F32)


def dot_nt(a, b):
    return lax.dot_general(a, b, (((1,), (1,)), ((), ())), preferred_element_type=F32)


def remote(src, dst, ssem, rsem, dev):
    return pltpu.make_async_remote_copy(src_ref=src, dst_ref=dst, send_sem=ssem, recv_sem=rsem,
                                        device_id=(dev,), device_id_type=MESH_ID)


def block_kernel(cfg, *refs):
    T, D, F, C = cfg
    F2 = 2 * F
    R = NDEV * C
    NT = -(-F // 128)
    FP = NT * 128
    (x_ref, dy_ref, wr_ref, br_ref, eid_ref, sid_ref, wgu_ref, bgu_ref, wd_ref, bd_ref,
     out_ref, dx_ref, dwr_ref, dbr_ref, dbd_ref, dbgu_ref, rx_o, q_o, a_o, dh_o,
     xall, dyall, yret, pret,
     wgu, wd, rx, rq, gs, us, asc, dh, yv, pv, xs, xv, dyv, acc, meta, dlall, mcol, emat,
     ag_s, ag_r, co_s, co_r, ya_s, ya_r, pa_s, pa_r, me_s, me_r, dl_s, dl_r, loc, tile_sem) = refs
    me = lax.axis_index("ep")
    lane = lambda shape: lax.broadcasted_iota(jnp.int32, shape, 1)
    sub = lambda shape: lax.broadcasted_iota(jnp.int32, shape, 0)

    ld_x = pltpu.make_async_copy(x_ref, xv, loc.at[0]); ld_x.start()
    ld_dy = pltpu.make_async_copy(dy_ref, dyv, loc.at[1]); ld_dy.start()
    ld_gu = pltpu.make_async_copy(wgu_ref, wgu, loc.at[2]); ld_gu.start()
    ld_d = pltpu.make_async_copy(wd_ref, wd.at[pl.ds(0, F)], loc.at[3]); ld_d.start()

    bar = pltpu.get_barrier_semaphore()
    for m in range(1, NDEV):
        pl.semaphore_signal(bar, inc=1, device_id=(flip(me, m),), device_id_type=MESH_ID)
    pl.semaphore_wait(bar, NDEV - 1)

    cuts = [0, 11 * D // 32, 22 * D // 32, D]
    srcs, alls = (x_ref, dy_ref), (xall, dyall)

    def offs(j):
        a, b, c = DIMS[j], DIMS[(j + 1) % 3], DIMS[(j + 2) % 3]
        return (a, b, c), (a, b, b ^ a, c, c ^ a, c ^ b, c ^ a ^ b)

    def cols(j):
        return pl.ds(cuts[j], cuts[j + 1] - cuts[j])

    def ag_copy(w, j, stage, t):
        order, _ = offs(j)
        tgt = order[stage]
        off = (0, order[0], order[1], order[0] ^ order[1])[t]
        idx = (0, 1, 3)[stage] + t
        shard = flip(me, off)
        src = srcs[w].at[:, cols(j)] if off == 0 else alls[w].at[shard, :, cols(j)]
        return remote(src, alls[w].at[shard, :, cols(j)], ag_s.at[w, j, idx], ag_r.at[w, j, idx], flip(me, tgt))

    def co_copy(w, j, idx):
        _, off = offs(j)
        shard = flip(me, off[idx])
        return remote(alls[w].at[shard, :, cols(j)], alls[w].at[shard, :, cols(j)],
                      co_s.at[w, j, idx], co_r.at[w, j, idx], flip(me, 1))

    def co_own(w):
        return remote(srcs[w], alls[w].at[me], co_s.at[w, 0, 7], co_r.at[w, 0, 7], flip(me, 1))

    def ag_send(w, stage):
        for t in range((1, 2, 4)[stage]):
            for j in range(3):
                ag_copy(w, j, stage, t).start()

    def ag_arrive(w, stage):
        for t in range((1, 2, 4)[stage]):
            for j in range(3):
                ag_copy(w, j, stage, t).wait_recv()

    def co_send(w, stage):
        for t in range((1, 2, 4)[stage]):
            for j in range(3):
                co_copy(w, j, (0, 1, 3)[stage] + t).start()

    def co_arrive(w):
        for idx in range(7):
            for j in range(3):
                co_copy(w, j, idx).wait_recv()
        co_own(w).wait_recv()

    ag_send(0, 0)
    ag_send(1, 0)
    co_own(0).start()
    co_own(1).start()

    ld_x.wait()
    st_x = pltpu.make_async_copy(xv, xall.at[me], loc.at[4]); st_x.start()
    logits = dot(xv[...], wr_ref[...]) + br_ref[...]
    eid, sid = eid_ref[...], sid_ref[...]
    experts = lane((T, NDEV))
    pick = [jnp.sum(jnp.where(eid[:, k:k + 1] == experts, logits, 0.0), axis=1, keepdims=True) for k in range(4)]
    top = functools.reduce(jnp.maximum, pick)
    ex = [jnp.exp(v - top) for v in pick]
    den = ex[0] + ex[1] + ex[2] + ex[3]
    gate = [v / den for v in ex]
    code = [jnp.where(sid[:, k:k + 1] >= 0, eid[:, k:k + 1] * C + sid[:, k:k + 1], -1).astype(F32) for k in range(4)]
    ln = lane((T, 128))
    packed = jnp.zeros((T, 128), F32)
    for k in range(4):
        packed = jnp.where(ln == k, code[k], packed)
        packed = jnp.where(ln == 4 + k, gate[k], packed)
    mcol[...] = packed
    meta[me] = packed.T[:8]
    er, ec = sub((256, 256)), lane((256, 256))
    emat[...] = jnp.where(jnp.where(ec < 128, 2 * ec, 2 * (ec - 128) + 1) == er, 1.0, 0.0).astype(BF)
    wd[pl.ds(F, FP - F), :] = jnp.zeros((FP - F, D), BF)
    ld_dy.wait()
    st_dy = pltpu.make_async_copy(dyv, dyall.at[me], loc.at[5]); st_dy.start()

    def meta_copy(m):
        return remote(meta.at[me], meta.at[me], me_s.at[m], me_r.at[m], flip(me, m))

    ag_arrive(0, 0)
    ag_send(0, 1)
    co_send(0, 0)
    for m in range(1, NDEV):
        meta_copy(m).start()
    ag_arrive(1, 0)
    ag_send(1, 1)
    co_send(1, 0)
    ag_arrive(0, 1)
    ag_send(0, 2)
    co_send(0, 1)
    ag_arrive(1, 1)
    ag_send(1, 2)
    co_send(1, 1)
    st_x.wait()
    st_dy.wait()
    for m in range(1, NDEV):
        remote(meta.at[me], meta.at[flip(me, m)], me_s.at[m], me_r.at[m], flip(me, m)).wait_recv()
    ld_gu.wait()
    ld_d.wait()
    ag_arrive(0, 2)
    co_send(0, 2)
    co_arrive(0)

    want = (me * C + sub((C, T))).astype(F32)

    def onehot(s):
        mt = meta[s]
        hit = jnp.zeros((C, T), F32)
        wsum = jnp.zeros((C, T), F32)
        for k in range(4):
            eq = want == mt[k:k + 1]
            hit = jnp.where(eq, 1.0, hit)
            wsum = jnp.where(eq, mt[4 + k:5 + k], wsum)
        return hit.astype(BF), wsum

    def shard_loop(src, body):
        def fetch(s, slot):
            return pltpu.make_async_copy(src.at[s], xs.at[slot], tile_sem.at[slot])
        fetch(0, 0).start()

        def step(s, carry):
            slot = lax.rem(s, 2)

            @pl.when(s + 1 < NDEV)
            def _():
                fetch(s + 1, 1 - slot).start()
            fetch(s, slot).wait()
            body(s, slot)
            return carry
        lax.fori_loop(0, NDEV, step, 0)

    CW = 1024

    def take_x(s, slot):
        hit, _ = onehot(s)
        row = pl.multiple_of(s * C, 16)
        for c in range(D // CW):
            rx[pl.ds(row, C), c * CW:(c + 1) * CW] = dot(hit, xs[slot, :, c * CW:(c + 1) * CW]).astype(BF)

    def take_q(s, slot):
        hit, wsum = onehot(s)
        wrow = jnp.sum(wsum, axis=1, keepdims=True)
        row = pl.multiple_of(s * C, 16)
        for c in range(D // CW):
            got = dot(hit, xs[slot, :, c * CW:(c + 1) * CW])
            rq[pl.ds(row, C), c * CW:(c + 1) * CW] = (wrow * got).astype(BF)

    shard_loop(xall, take_x)
    MB = 256

    def fwd_tile(m, n, width):
        rows = pl.ds(pl.multiple_of(m * MB, MB), MB)
        wcol = pl.multiple_of(n * 256, 256) if not isinstance(n, int) else n * 256
        h = dot(rx[rows, :], wgu[:, pl.ds(wcol, width)])
        gu = jnp.zeros((MB, 256), F32)
        for part in split3(h):
            gu = gu + dot(part, emat[:width, :])
        gu = gu + bgu_ref[n]
        g, u = gu[:, :128], gu[:, 128:]
        gc = jnp.minimum(g, SWIGLU_LIMIT)
        uc = jnp.clip(u, -SWIGLU_LIMIT, SWIGLU_LIMIT)
        act = gc * jax.nn.sigmoid(SWIGLU_ALPHA * gc) * (uc + 1.0)
        acol = pl.multiple_of(n * 128, 128) if not isinstance(n, int) else n * 128
        gs[rows, pl.ds(acol, 128)] = g
        us[rows, pl.ds(acol, 128)] = u
        asc[rows, pl.ds(acol, 128)] = act.astype(BF)

    def bwd_tile(m, n, width):
        rows = pl.ds(pl.multiple_of(m * MB, MB), MB)
        acol = pl.multiple_of(n * 128, 128) if not isinstance(n, int) else n * 128
        wcol = pl.multiple_of(n * 256, 256) if not isinstance(n, int) else n * 256
        da = dot_nt(rq[rows, :], wd[pl.ds(acol, 128), :])
        g, u = gs[rows, pl.ds(acol, 128)], us[rows, pl.ds(acol, 128)]
        gc = jnp.minimum(g, SWIGLU_LIMIT)
        uc = jnp.clip(u, -SWIGLU_LIMIT, SWIGLU_LIMIT)
        sg = jax.nn.sigmoid(SWIGLU_ALPHA * gc)
        glu = gc * sg
        dg = da * (uc + 1.0) * (sg + SWIGLU_ALPHA * glu * (1.0 - sg))
        du = da * glu
        au = jnp.abs(u)
        dg = dg * jnp.where(g < SWIGLU_LIMIT, 1.0, jnp.where(g > SWIGLU_LIMIT, 0.0, 0.5))
        du = du * jnp.where(au < SWIGLU_LIMIT, 1.0, jnp.where(au > SWIGLU_LIMIT, 0.0, 0.5))
        pair = jnp.concatenate([dg.astype(BF), du.astype(BF)], axis=1)
        dh[rows, pl.ds(wcol, width)] = dot_nt(pair, emat[:width, :]).astype(BF)

    def tiles(fn):
        full = F2 // 256

        def row_step(m, carry):
            def step(n, c):
                fn(m, n, 256)
                return c
            lax.fori_loop(0, full, step, 0)
            if F2 % 256:
                fn(m, full, F2 % 256)
            return carry
        lax.fori_loop(0, R // MB, row_step, 0)

    tiles(fwd_tile)
    YW = 256

    def y_step(i, carry):
        m, n = lax.div(i, D // YW), lax.rem(i, D // YW)
        rows = pl.ds(pl.multiple_of(m * MB, MB), MB)
        col = pl.ds(pl.multiple_of(n * YW, YW), YW)
        yv[rows, col] = (dot(asc[rows, :], wd[:, col]) + bd_ref[:, col]).astype(BF)
        return carry
    lax.fori_loop(0, (R // MB) * (D // YW), y_step, 0)

    order = [c * 2 + k for c in CHIP_ORDER for k in (0, 1)]
    order.insert(0, 1)

    def ret_copy(buf, dst, ss, rs, m):
        d = flip(me, m)
        return remote(buf.at[pl.ds(d * C, C)], dst.at[me], ss.at[m], rs.at[m], d)

    for m in order:
        ret_copy(yv, yret, ya_s, ya_r, m).start()
    st = [pltpu.make_async_copy(rx, rx_o, loc.at[6]), pltpu.make_async_copy(asc, a_o, loc.at[7])]
    for s in st:
        s.start()

    ag_arrive(1, 2)
    co_send(1, 2)
    co_arrive(1)
    shard_loop(dyall, take_q)
    tiles(bwd_tile)

    def p_step(i, carry):
        m, n = lax.div(i, D // YW), lax.rem(i, D // YW)
        rows = pl.ds(pl.multiple_of(m * MB, MB), MB)
        off = pl.ds(pl.multiple_of(n * YW, YW), YW)
        pv[rows, off] = dot_nt(dh[rows, :], wgu[off, :]).astype(BF)
        return carry
    lax.fori_loop(0, (R // MB) * (D // YW), p_step, 0)
    early, late = order[:-2], order[-2:]
    for m in early:
        ret_copy(pv, pret, pa_s, pa_r, m).start()
    st += [pltpu.make_async_copy(rq, q_o, loc.at[8]), pltpu.make_async_copy(dh, dh_o, loc.at[9])]
    for s in st[2:]:
        s.start()
    ones = jnp.ones((8, R), BF)

    def bd_step(n, carry):
        col = pl.ds(pl.multiple_of(n * 512, 512), 512)
        dbd_ref[:, col] = dot(ones, rq[:, col])
        return carry
    lax.fori_loop(0, D // 512, bd_step, 0)
    dbgu_ref[...] = dot(ones, dh[...])

    def get_cols():
        pk = mcol[...]
        return [pk[:, k:k + 1] for k in range(4)], [pk[:, 4 + k:5 + k] for k in range(4)]

    def hits(e):
        cd, gt = get_cols()
        pos = (e * C + lane((T, C))).astype(F32)
        return [cd[k] == pos for k in range(4)], gt

    def ret_loop(buf, dst, rs, first, body, carry):
        def fetch(i, slot):
            e = flip(me, i)
            return pltpu.make_async_copy(dst.at[e], xs.at[slot, pl.ds(0, C)], tile_sem.at[slot])

        def arrived(m):
            e = flip(me, m)
            return remote(buf.at[pl.ds(e * C, C)], dst.at[e], ya_s.at[0], rs.at[m], e)
        for m in order:
            arrived(m).wait_recv()
        own = pltpu.make_async_copy(buf.at[pl.ds(me * C, C)], dst.at[me], loc.at[first])
        own.start()
        own.wait()
        fetch(0, 0).start()

        def step(i, c):
            slot = lax.rem(i, 2)

            @pl.when(i + 1 < NDEV)
            def _():
                fetch(i + 1, 1 - slot).start()
            fetch(i, slot).wait()
            return body(flip(me, i), slot, c)
        return lax.fori_loop(0, NDEV, step, carry)

    acc[...] = jnp.zeros((T, D), F32)

    def add_y(e, slot, rs):
        hk, gt = hits(e)
        cw = jnp.zeros((T, C), F32)
        for k in range(4):
            cw = jnp.where(hk[k], gt[k], cw)
        c3 = jnp.concatenate(split3(cw), axis=0)
        for c in range(D // CW):
            cc = slice(c * CW, (c + 1) * CW)
            v = dot(c3, xs[slot, :C, cc])
            acc[:, cc] += v[:T] + v[T:2 * T] + v[2 * T:]
        rm = dot_nt(dyv[...], xs[slot, :C, :])
        return tuple(rs[k] + jnp.sum(jnp.where(hk[k], rm, 0.0), axis=1, keepdims=True) for k in range(4))

    zero = jnp.zeros((T, 1), F32)
    rk = ret_loop(yv, yret, ya_r, 10, add_y, (zero,) * 4)
    out_ref[...] = acc[...].astype(BF)
    _, gt = get_cols()
    mean = gt[0] * rk[0] + gt[1] * rk[1] + gt[2] * rk[2] + gt[3] * rk[3]
    eid = eid_ref[...]
    dl = jnp.zeros((T, 128), F32)
    for k in range(4):
        dl = jnp.where(eid[:, k:k + 1] == ln, gt[k] * (rk[k] - mean), dl)
    dlall[me] = dl.T[:NDEV].astype(BF)
    dlb = dl.astype(BF)[:, :NDEV]
    for c in range(D // CW):
        cc = slice(c * CW, (c + 1) * CW)
        acc[:, cc] = dot_nt(dlb, wr_ref[cc, :])

    def dl_copy(m):
        return remote(dlall.at[me], dlall.at[me], dl_s.at[m], dl_r.at[m], flip(me, m))

    for m in range(1, NDEV):
        dl_copy(m).start()
    for m in late:
        ret_copy(pv, pret, pa_s, pa_r, m).start()

    for m in range(1, NDEV):
        e = flip(me, m)
        remote(dlall.at[me], dlall.at[e], dl_s.at[m], dl_r.at[m], e).wait_recv()
    dwr_ref[...] = jnp.zeros(dwr_ref.shape, F32)
    dbr_ref[...] = jnp.zeros(dbr_ref.shape, F32)

    def add_wr(s, slot):
        dls = dlall[s]
        dbr_ref[...] += dls.astype(F32)
        for c in range(D // CW):
            cc = slice(c * CW, (c + 1) * CW)
            dwr_ref[:, cc] += dot(dls, xs[slot, :, cc])
    shard_loop(xall, add_wr)

    def add_p(e, slot, carry):
        hk, _ = hits(e)
        hit = jnp.zeros((T, C), F32)
        for k in range(4):
            hit = jnp.where(hk[k], 1.0, hit)
        hb = hit.astype(BF)
        for c in range(D // CW):
            cc = slice(c * CW, (c + 1) * CW)
            acc[:, cc] += dot(hb, xs[slot, :C, cc])
        return carry
    ret_loop(pv, pret, pa_r, 11, add_p, 0)
    dx_ref[...] = acc[...].astype(BF)

    for w in range(2):
        co_own(w).wait_send()
        for j in range(3):
            for stage in range(3):
                for t in range((1, 2, 4)[stage]):
                    ag_copy(w, j, stage, t).wait_send()
            for idx in range(7):
                co_copy(w, j, idx).wait_send()
    for m in range(1, NDEV):
        meta_copy(m).wait_send()
        dl_copy(m).wait_send()
        ret_copy(yv, yret, ya_s, ya_r, m).wait_send()
        ret_copy(pv, pret, pa_s, pa_r, m).wait_send()
    for s in st:
        s.wait()


def solution(mesh):
    def local_block(hidden, grad_out, w_router, b_router, expert_ids, slot_ids, w_gate_up, b_gate_up, w_down, b_down):
        T, D = hidden.shape
        F = w_down.shape[1]
        C = (3 * T * 4 + 2 * NDEV - 1) // (2 * NDEV)
        R = NDEV * C
        NT = -(-F // 128)
        FP = NT * 128
        bias = jnp.pad(b_gate_up.reshape(F, 2), ((0, FP - F), (0, 0))).reshape(NT, 128, 2)
        bias = bias.transpose(0, 2, 1).reshape(NT, 1, 256)
        S = jax.ShapeDtypeStruct
        vm, hb = pl.BlockSpec(memory_space=pltpu.VMEM), pl.BlockSpec(memory_space=pl.ANY)
        outs = [S((T, D), BF), S((T, D), BF), S((NDEV, D), F32), S((NDEV, T), F32), S((8, D), F32), S((8, 2 * F), F32),
                S((R, D), BF), S((R, D), BF), S((R, FP), BF), S((R, 2 * F), BF),
                S((NDEV, T, D), BF), S((NDEV, T, D), BF), S((NDEV, C, D), BF), S((NDEV, C, D), BF)]
        V, dma = pltpu.VMEM, pltpu.SemaphoreType.DMA
        scratch = [V((D, 2 * F), BF), V((FP, D), BF), V((R, D), BF), V((R, D), BF), V((R, FP), F32), V((R, FP), F32),
                   V((R, FP), BF), V((R, 2 * F), BF), V((R, D), BF), V((R, D), BF), V((2, T, D), BF), V((T, D), BF),
                   V((T, D), BF), V((T, D), F32), V((NDEV, 8, T), F32), V((NDEV, NDEV, T), BF), V((T, 128), F32),
                   V((256, 256), BF),
                   dma((2, 3, 7)), dma((2, 3, 7)), dma((2, 3, 8)), dma((2, 3, 8)),
                   dma((16,)), dma((16,)), dma((16,)), dma((16,)), dma((16,)), dma((16,)), dma((16,)), dma((16,)),
                   dma((12,)), dma((2,))]
        res = pl.pallas_call(
            functools.partial(block_kernel, (T, D, F, C)),
            out_shape=outs,
            in_specs=[hb, hb, vm, vm, vm, vm, hb, vm, hb, vm],
            out_specs=[vm, vm, vm, vm, vm, vm] + [hb] * 8,
            scratch_shapes=scratch,
            compiler_params=pltpu.CompilerParams(collective_id=0, has_side_effects=True, vmem_limit_bytes=67043328),
            name="moe_block",
        )(hidden, grad_out, w_router, b_router.reshape(1, NDEV), expert_ids, slot_ids,
          w_gate_up[0], bias, w_down[0], b_down)
        out, dx, dwr, dbr, dbd, dbgu, rx, q, a, dh = res[:10]
        grad_w_down = jnp.einsum('rf,rd->fd', a[:, :F], q, preferred_element_type=F32)[None]
        grad_w_gate_up = jnp.einsum('rd,rf->df', rx, dh, preferred_element_type=F32)[None]
        return (out, dx, dwr.T, jnp.sum(dbr, axis=1), grad_w_gate_up, dbgu[:1], grad_w_down, dbd[:1])

    tok = P('ep', None)
    ex3, ex2 = P('ep', None, None), P('ep', None)
    in_specs = (tok, tok, P(None, None), P(None), tok, tok, ex3, ex2, ex3, ex2)
    out_specs = (tok, tok, P(None, None), P(None), ex3, ex2, ex3, ex2)
    return jax.shard_map(local_block, mesh=mesh, in_specs=in_specs, out_specs=out_specs, check_vma=False)
```

time: 630 us -> 363 us (0.58)
  Pallas kernels: 0 us -> 307 us
  waiting for transfers between devices: 231 us -> 0 us
  blocking collectives: 107 us -> 0 us
  local copies, waits for them, and re-layouts: 122 us -> 26.9 us
  matrix products: 91.2 us -> 24.6 us
  other arithmetic: 39 us -> 2.03 us
  starting transfers between devices: 19.6 us -> 0 us
  between operations: 14.7 us -> 0.69 us
    pallas_call x0 -> x1, Pallas kernels: none -> 307 us  [local_block(): pl.pallas_call(functools.partial(block_kernel, (T, D, F, C)), out_shape=o...]
    all_to_all x4 -> x0, waiting for transfers between devices: 231 us -> none  [the longest x1 80.4 us: local_block(): lax.all_to_all(send_q, 'ep', 0, 0, tiled=True)]
    psum x1 -> x0, blocking collectives: 107 us -> none  [local_block(): lax.psum(jnp.sum(logit_grad, axis=0, dtype=jnp.float32), 'ep')]
    gather x12 -> x0, local copies, waits for them, and re-layouts: 67.4 us -> none  [the longest x2 19.6 us: local_block(): p_copies = jnp.take(back_p, dest_row, axis=0, mode='fill', fill_value=0)]
    dot_general x10 -> x2, matrix products: 91.2 us -> 24.6 us  [the longest x1 12.3 us: local_block(): jnp.einsum('rd,rf->df', rx, dh, preferred_element_type=F32)[None]]
    reduce_sum x7 -> x1, other arithmetic: 22.5 us -> 1.32 us  [local_block(): jnp.sum(dbr, axis=1)]
    all_to_all x4 -> x0, starting transfers between devices: 19.5 us -> none  [the longest x1 5.56 us: local_block(): lax.all_to_all(send_x, 'ep', 0, 0, tiled=True)]
    convert_element_type x2 -> x0, local copies, waits for them, and re-layouts: 16.9 us -> none  [local_block(): pre_grad = act_vjp(act_grad)[0].astype(jnp.bfloat16)]
  transfers between devices with their start and end apart: 5 -> 0, of which waited for: 3 -> 0; matrix products, arithmetic and copies ran while one was open for 13% -> 0% of each run, Pallas kernels for 0% -> 0%
where the time goes in v1:
time: 363 us; the launch traced here: 361 us
  Pallas kernels  307 us (85%)
  local copies, waits for them, and re-layouts  26.9 us (7%)
  matrix products  24.6 us (7%)
    pallas_call x1, Pallas kernels, local_block(): pl.pallas_call(functools.partial(block_kernel, (T, D, F, C)), out_shape=o...  307 us
    unnamed x17, local copies, waits for them, and re-layouts  23 us
    dot_general x1, matrix products, local_block(): jnp.einsum('rd,rf->df', rx, dh, preferred_element_type=F32)[None]  12.3 us
    dot_general x1, matrix products, local_block(): jnp.einsum('rf,rd->fd', a[:, :F], q, preferred_element_type=F32)[None]  12.2 us

profile of v1, /device:TPU:0, one launch (start us, length us, event | category | flops | bytes accessed | tf_op | source)
XLA Modules:
  0.0 361.4 jit_solution(9521655646642921747)
XLA Ops:
  0.6 0.7 reduce
  1.3 1.4 copy.26.refs_4_
  2.8 1.4 copy.27.refs_5_
  4.2 0.3 reshape.29
  4.5 0.7 copy.24
  5.3 2.2 copy.25.refs_2_
  7.5 15.3 %copy.22 = bf16[1,4096,1376]{2,1,0:T(8,128)(2,1)} copy(bf16[1,4096,1376]{1,2,0:T(8,128)(2,1)} %param.16) | data formatting | bytes 22544384 | tf_op args[6]
  22.8 307.2 %moe_block.1 = (bf16[128,4096]{1,0:T(8,128)(2,1)}, bf16[128,4096]{1,0:T(8,128)(2,1)}, f32[16,4096]{1,0:T(8,128)}, f32[16,128]{1,0:T(8,128)}, f32[8,4096]{1,0:T(8...) custom-call(bf16[128,4096]{1,0:T(8,128)(2,1)} %refs_0_.1, ...), custom_call_target="tpu_custom_call" | custom-call | tf_op jit(solution)/shard_map/moe_block/pallas_call | solution.py:471
  329.9 1.3 reduce_sum.9
  331.2 1.4 slice.9
  332.6 1.5 slice.11
  334.1 0.0 copy-start.3
  334.1 0.0 copy-start.4
  334.1 12.2 %convolution_bitcast_fusion.1 = f32[1,688,4096]{2,1,0:T(8,128)} fusion(bf16[768,4096]{1,0:T(8,128)(2,1)} %get-tuple-element.26, bf16[768,768]{1,0:T(8,128)(2,1)} %get-tuple-element.25), kind=kOutput, calls=%fused_computation.1 | convolution fusion | flops 4328521728 | bytes 18743296 | tf_op jit(solution)/shard_map/rf,rd->fd/dot_general | solution.py:482
  346.4 0.0 copy-done.3
  346.4 0.0 copy-done.4
  346.4 0.0 copy-start.1
  346.4 0.0 copy-start
  346.4 0.0 copy-start.2
  346.4 12.3 %convolution_bitcast_fusion = f32[1,4096,1376]{1,2,0:T(8,128)} fusion(bf16[768,4096]{1,0:T(8,128)(2,1)S(1)} %copy-done.3, bf16[768,1376]{1,0:T(8,128)(2,1)S(1)} %copy-done.4), kind=kOutput, calls=%fused_computation | convolution fusion | flops 8657043456 | bytes 30949376 | tf_op jit(solution)/shard_map/rd,rf->df/dot_general | solution.py:483
  358.7 0.0 copy-done.1
  358.7 1.0 copy.33
  359.7 0.0 copy-done
  359.7 1.0 copy.34
  360.7 0.0 copy-done.2
  360.7 0.7 copy.35
  (1 shorter events, 0.0 us)
Async XLA Ops:
  334.1 12.2 %copy-start.3 = (bf16[768,4096]{1,0:T(8,128)(2,1)S(1)}, bf16[768,4096]{1,0:T(8,128)(2,1)}, u32[]{:S(2)}) copy-start(bf16[768,4096]{1,0:T(8,128)(2,1)} %get-tuple-element.22) | copy-start | bytes 18874372
  334.1 12.2 %copy-start.4 = (bf16[768,1376]{1,0:T(8,128)(2,1)S(1)}, bf16[768,1376]{1,0:T(8,128)(2,1)}, u32[]{:S(2)}) copy-start(bf16[768,1376]{1,0:T(8,128)(2,1)} %get-tuple-element.23) | copy-start | bytes 6340612
  346.4 12.3 %copy-start.1 = (bf16[128,4096]{1,0:T(8,128)(2,1)S(1)}, bf16[128,4096]{1,0:T(8,128)(2,1)}, u32[]{:S(2)}) copy-start(bf16[128,4096]{1,0:T(8,128)(2,1)} %get-tuple-element.36) | copy-start | bytes 3145732
  346.4 13.3 %copy-start = (bf16[128,4096]{1,0:T(8,128)(2,1)S(1)}, bf16[128,4096]{1,0:T(8,128)(2,1)}, u32[]{:S(2)}) copy-start(bf16[128,4096]{1,0:T(8,128)(2,1)} %get-tuple-element.37) | copy-start | bytes 3145732
  346.4 14.3 %copy-start.2 = (f32[16,4096]{1,0:T(8,128)S(1)}, f32[16,4096]{1,0:T(8,128)}, u32[]{:S(2)}) copy-start(f32[16,4096]{1,0:T(8,128)} %get-tuple-element.20) | copy-start | bytes 786436

commit v2 on v1

v2 whole, which is shorter than its diff:
```python
import functools

import jax
import jax.numpy as jnp
from jax import lax
from jax.experimental import pallas as pl
from jax.experimental.pallas import tpu as pltpu
from jax.sharding import PartitionSpec as P

SWIGLU_LIMIT = 7.0
SWIGLU_ALPHA = 1.702
MESH_ID = pl.DeviceIdType.MESH
BF = jnp.bfloat16
F32 = jnp.float32

DIMS = (2, 4, 8)
CHIP_ORDER = (3, 4, 5, 2, 6, 1, 7)
NDEV = 16


def flip(me, mask):
    out = 0
    for b in (1, 2, 4, 8):
        bit = lax.rem(lax.div(me, b), 2)
        if isinstance(mask, int):
            if mask & b:
                bit = 1 - bit
        else:
            bit = lax.rem(bit + lax.rem(lax.div(mask, b), 2), 2)
        out = out + b * bit
    return out


def split3(v):
    hi = v.astype(BF)
    rest = v - hi.astype(F32)
    mid = rest.astype(BF)
    low = (rest - mid.astype(F32)).astype(BF)
    return hi, mid, low


def dot(a, b):
    return jnp.dot(a, b, preferred_element_type=F32)


def dot_nt(a, b):
    return lax.dot_general(a, b, (((1,), (1,)), ((), ())), preferred_element_type=F32)


def remote(src, dst, ssem, rsem, dev):
    return pltpu.make_async_remote_copy(src_ref=src, dst_ref=dst, send_sem=ssem, recv_sem=rsem,
                                        device_id=(dev,), device_id_type=MESH_ID)


def block_kernel(cfg, *refs):
    T, D, F, C = cfg
    F2 = 2 * F
    R = NDEV * C
    NT = -(-F // 128)
    FP = NT * 128
    (x_ref, dy_ref, wr_ref, br_ref, eid_ref, sid_ref, wgu_ref, bgu_ref, wd_ref, bd_ref,
     out_ref, dx_ref, dwr_ref, dbr_ref, dbd_ref, dbgu_ref, rx_o, q_o, a_o, dh_o,
     xall, dyall, yret, pret,
     wgu, wd, rx, rq, gs, us, asc, dh, yv, pv, xs, xv, dyv, acc, meta, dlall, mcol, emat, wpart,
     ag_s, ag_r, co_s, co_r, lf_s, lf_r, ya_s, ya_r, pa_s, pa_r, me_s, me_r, dl_s, dl_r, wr_s, wr_r,
     loc, tile_sem) = refs
    me = lax.axis_index("ep")
    core = lax.rem(me, 2)
    lane = lambda shape: lax.broadcasted_iota(jnp.int32, shape, 1)
    sub = lambda shape: lax.broadcasted_iota(jnp.int32, shape, 0)

    ld_x = pltpu.make_async_copy(x_ref, xv, loc.at[0]); ld_x.start()
    ld_dy = pltpu.make_async_copy(dy_ref, dyv, loc.at[1]); ld_dy.start()
    ld_gu = pltpu.make_async_copy(wgu_ref, wgu, loc.at[2]); ld_gu.start()
    ld_d = pltpu.make_async_copy(wd_ref, wd.at[pl.ds(0, F)], loc.at[3]); ld_d.start()

    bar = pltpu.get_barrier_semaphore()
    for m in range(1, NDEV):
        pl.semaphore_signal(bar, inc=1, device_id=(flip(me, m),), device_id_type=MESH_ID)
    pl.semaphore_wait(bar, NDEV - 1)

    cuts = [0, 11 * D // 32, 22 * D // 32, D]
    srcs, alls, rows_of, stage_of = (x_ref, dy_ref), (xall, dyall), (rx, rq), (yv, pv)
    local = (xv, dyv)
    dims = [(DIMS[j], DIMS[(j + 1) % 3], DIMS[(j + 2) % 3]) for j in range(3)]
    plane = [(0, a, b, a ^ b) for a, b, _ in dims]

    def cols(j):
        return pl.ds(cuts[j], cuts[j + 1] - cuts[j])

    def ag_copy(w, j, idx):
        a, b, _ = dims[j]
        off = (0, 0, a)[idx]
        shard = flip(me, off)
        src = srcs[w].at[:, cols(j)] if off == 0 else alls[w].at[shard, :, cols(j)]
        return remote(src, alls[w].at[shard, :, cols(j)], ag_s.at[w, j, idx], ag_r.at[w, j, idx],
                      flip(me, (a, b, b)[idx]))

    def co_copy(w, j, t):
        shard = flip(me, plane[j][t])
        src = srcs[w].at[:, cols(j)] if t == 0 else alls[w].at[shard, :, cols(j)]
        return remote(src, alls[w].at[shard, :, cols(j)], co_s.at[w, j, t], co_r.at[w, j, t], flip(me, 1))

    def lf_copy(w, j, t, k):
        shard = flip(me, plane[j][t])
        there = lax.div(flip(me, dims[j][2]), 2) * 2
        return remote(stage_of[w].at[pl.ds(t * 2 * C + k * C, C), cols(j)],
                      rows_of[w].at[pl.ds(pl.multiple_of(shard * C, 16), C), cols(j)],
                      lf_s.at[w, j, t, k], lf_r.at[w, j, t, core], there + k)

    def lf_arrive(w):
        for t in range(4):
            for j in range(3):
                there = lax.div(flip(me, dims[j][2]), 2) * 2
                for k in range(2):
                    shard = flip(there + k, plane[j][t])
                    remote(stage_of[w].at[pl.ds(t * 2 * C + k * C, C), cols(j)],
                           rows_of[w].at[pl.ds(pl.multiple_of(shard * C, 16), C), cols(j)],
                           lf_s.at[w, j, t, k], lf_r.at[w, j, t, k], there + k).wait_recv()

    def compact(w, j, t, s, src, leaf):
        mt = meta[s]
        M = 3 * C if leaf else C
        pos = sub((M, T))
        want = me * C + pos
        if leaf:
            there = lax.div(flip(me, dims[j][2]), 2) * 2
            want = jnp.where(pos < C, want, there * C + pos - C)
        want = want.astype(F32)
        hit = jnp.zeros((M, T), F32)
        wsum = jnp.zeros((M, T), F32)
        for k in range(4):
            eq = want == mt[k:k + 1]
            hit = jnp.where(eq, 1.0, hit)
            if w:
                wsum = jnp.where(eq, mt[4 + k:5 + k], wsum)
        hb = hit.astype(BF)
        wrow = jnp.sum(wsum, axis=1, keepdims=True)
        row = pl.multiple_of(s * C, 16)
        c0 = cuts[j]
        while c0 < cuts[j + 1]:
            c1 = min(c0 + 512, cuts[j + 1])
            got = dot(hb, src[:, c0:c1])
            if w:
                got = wrow * got
            got = got.astype(BF)
            rows_of[w][pl.ds(row, C), c0:c1] = got[:C]
            if leaf:
                stage_of[w][t * 2 * C:(t + 1) * 2 * C, c0:c1] = got[C:]
            c0 = c1

    def load_part(w, j, s, slot):
        return pltpu.make_async_copy(alls[w].at[s, :, cols(j)], xs.at[slot, :, cols(j)], tile_sem.at[slot, j])

    def issue_own(w):
        for idx in (0, 1):
            for j in range(3):
                ag_copy(w, j, idx).start()
        for j in range(3):
            co_copy(w, j, 0).start()

    def issue_leaf_own(w):
        for j in range(3):
            compact(w, j, 0, me, local[w], True)
            for k in range(2):
                lf_copy(w, j, 0, k).start()

    def relay(w, idx):
        slot = idx % 2
        t = idx + 1
        for j in range(3):
            ag_copy_in(w, j, idx).wait_recv()
            if idx == 0:
                ag_copy(w, j, 2).start()
            co_copy(w, j, t).start()
            load_part(w, j, flip(me, plane[j][t]), slot).start()
        for j in range(3):
            s = flip(me, plane[j][t])
            load_part(w, j, s, slot).wait()
            compact(w, j, t, s, xs.at[slot], True)
            for k in range(2):
                lf_copy(w, j, t, k).start()

    def ag_copy_in(w, j, idx):
        shard = flip(me, plane[j][idx + 1])
        a, b, _ = dims[j]
        return remote(srcs[w].at[:, cols(j)], alls[w].at[shard, :, cols(j)], ag_s.at[w, j, idx], ag_r.at[w, j, idx],
                      flip(me, (a, b, b)[idx]))

    def siblings(w):
        other = flip(me, 1)

        def begin(t):
            for j in range(3):
                shard = flip(other, plane[j][t])
                remote(srcs[w].at[:, cols(j)], alls[w].at[shard, :, cols(j)], co_s.at[w, j, t], co_r.at[w, j, t],
                       other).wait_recv()
                load_part(w, j, shard, t % 2).start()
        begin(0)
        for t in range(4):
            if t < 3:
                begin(t + 1)
            for j in range(3):
                shard = flip(other, plane[j][t])
                load_part(w, j, shard, t % 2).wait()
                compact(w, j, t, shard, xs.at[t % 2], False)

    issue_own(0)

    ld_x.wait()
    st_x = pltpu.make_async_copy(xv, xall.at[me], loc.at[4]); st_x.start()
    logits = dot_nt(wr_ref[...], xv[...]) + br_ref[...]
    eid, sid = eid_ref[...], sid_ref[...]
    experts = sub((NDEV, T))
    pick = [jnp.sum(jnp.where(eid[k:k + 1] == experts, logits, 0.0), axis=0, keepdims=True) for k in range(4)]
    top = functools.reduce(jnp.maximum, pick)
    ex = [jnp.exp(v - top) for v in pick]
    den = ex[0] + ex[1] + ex[2] + ex[3]
    sb = sub((T, T))
    packed = jnp.zeros((T, T), F32)
    for k in range(4):
        code = jnp.where(sid[k:k + 1] >= 0, eid[k:k + 1] * C + sid[k:k + 1], -1).astype(F32)
        packed = jnp.where(sb == k, code, packed)
        packed = jnp.where(sb == 4 + k, ex[k] / den, packed)
        packed = jnp.where(sb == 8 + k, eid[k:k + 1].astype(F32), packed)
    mcol[...] = packed.T
    meta[me] = packed[:8]
    er, ec = sub((256, 256)), lane((256, 256))
    emat[...] = jnp.where(jnp.where(ec < 128, 2 * ec, 2 * (ec - 128) + 1) == er, 1.0, 0.0).astype(BF)

    def meta_copy(m):
        return remote(meta.at[me], meta.at[me], me_s.at[m], me_r.at[m], flip(me, m))

    compact(0, 0, 0, me, local[0], True)
    for m in range(1, NDEV):
        meta_copy(m).start()
    issue_leaf_own(0)
    wd[pl.ds(F, FP - F), :] = jnp.zeros((FP - F, D), BF)
    for m in range(1, NDEV):
        remote(meta.at[me], meta.at[flip(me, m)], me_s.at[m], me_r.at[m], flip(me, m)).wait_recv()
    relay(0, 0)
    relay(0, 1)
    relay(0, 2)
    issue_own(1)
    ld_dy.wait()
    issue_leaf_own(1)
    siblings(0)
    st_x.wait()
    ld_gu.wait()
    ld_d.wait()
    lf_arrive(0)

    MB = 256

    def fwd_tile(m, n, width):
        rows = pl.ds(pl.multiple_of(m * MB, MB), MB)
        wrow = pl.multiple_of(n * 256, 256) if not isinstance(n, int) else n * 256
        h = dot_nt(rx[rows, :], wgu[pl.ds(wrow, width), :])
        gu = jnp.zeros((MB, 256), F32)
        for part in split3(h):
            gu = gu + dot(part, emat[:width, :])
        gu = gu + bgu_ref[n]
        g, u = gu[:, :128], gu[:, 128:]
        gc = jnp.minimum(g, SWIGLU_LIMIT)
        uc = jnp.clip(u, -SWIGLU_LIMIT, SWIGLU_LIMIT)
        act = gc * jax.nn.sigmoid(SWIGLU_ALPHA * gc) * (uc + 1.0)
        acol = pl.multiple_of(n * 128, 128) if not isinstance(n, int) else n * 128
        gs[rows, pl.ds(acol, 128)] = g
        us[rows, pl.ds(acol, 128)] = u
        asc[rows, pl.ds(acol, 128)] = act.astype(BF)

    def bwd_tile(m, n, width):
        rows = pl.ds(pl.multiple_of(m * MB, MB), MB)
        acol = pl.multiple_of(n * 128, 128) if not isinstance(n, int) else n * 128
        wcol = pl.multiple_of(n * 256, 256) if not isinstance(n, int) else n * 256
        da = dot_nt(rq[rows, :], wd[pl.ds(acol, 128), :])
        g, u = gs[rows, pl.ds(acol, 128)], us[rows, pl.ds(acol, 128)]
        gc = jnp.minimum(g, SWIGLU_LIMIT)
        uc = jnp.clip(u, -SWIGLU_LIMIT, SWIGLU_LIMIT)
        sg = jax.nn.sigmoid(SWIGLU_ALPHA * gc)
        glu = gc * sg
        dg = da * (uc + 1.0) * (sg + SWIGLU_ALPHA * glu * (1.0 - sg))
        du = da * glu
        au = jnp.abs(u)
        dg = dg * jnp.where(g < SWIGLU_LIMIT, 1.0, jnp.where(g > SWIGLU_LIMIT, 0.0, 0.5))
        du = du * jnp.where(au < SWIGLU_LIMIT, 1.0, jnp.where(au > SWIGLU_LIMIT, 0.0, 0.5))
        pair = jnp.concatenate([dg.astype(BF), du.astype(BF)], axis=1)
        dh[rows, pl.ds(wcol, width)] = dot_nt(pair, emat[:width, :]).astype(BF)

    def tiles(fn, lo, hi):
        full = F2 // 256

        def row_step(m, carry):
            def step(n, c):
                fn(m, n, 256)
                return c
            lax.fori_loop(0, full, step, 0)
            if F2 % 256:
                fn(m, full, F2 % 256)
            return carry
        lax.fori_loop(lo, hi, row_step, 0)

    YW = 256
    NY = D // YW

    def y_step(i, carry):
        m, n = lax.div(i, NY), lax.rem(i, NY)
        rows = pl.ds(pl.multiple_of(m * MB, MB), MB)
        col = pl.ds(pl.multiple_of(n * YW, YW), YW)
        yv[rows, col] = (dot(asc[rows, :], wd[:, col]) + bd_ref[:, col]).astype(BF)
        return carry

    tiles(fwd_tile, 0, 1)
    relay(1, 0)
    relay(1, 1)
    tiles(fwd_tile, 1, R // MB)
    for t in range(4):
        for j in range(3):
            for k in range(2):
                lf_copy(0, j, t, k).wait_send()
    lax.fori_loop(0, NY, y_step, 0)
    relay(1, 2)
    lax.fori_loop(NY, (R // MB) * NY, y_step, 0)

    order = [c * 2 + k for c in CHIP_ORDER for k in (0, 1)]
    order.insert(0, 1)

    def ret_copy(buf, dst, ss, rs, m):
        d = flip(me, m)
        return remote(buf.at[pl.ds(pl.multiple_of(d * C, 16), C)], dst.at[me], ss.at[m], rs.at[m], d)

    for m in order:
        ret_copy(yv, yret, ya_s, ya_r, m).start()
    st = [pltpu.make_async_copy(rx, rx_o, loc.at[6]), pltpu.make_async_copy(asc, a_o, loc.at[7])]
    for s in st:
        s.start()

    siblings(1)
    lf_arrive(1)
    tiles(bwd_tile, 0, R // MB)
    for t in range(4):
        for j in range(3):
            for k in range(2):
                lf_copy(1, j, t, k).wait_send()

    def p_step(i, carry):
        m, n = lax.div(i, NY), lax.rem(i, NY)
        rows = pl.ds(pl.multiple_of(m * MB, MB), MB)
        col = pl.ds(pl.multiple_of(n * YW, YW), YW)
        pv[rows, col] = dot(dh[rows, :], wgu[:, col]).astype(BF)
        return carry
    lax.fori_loop(0, (R // MB) * NY, p_step, 0)
    first, second, last = order[:5], order[5:13], order[13:]
    for m in first:
        ret_copy(pv, pret, pa_s, pa_r, m).start()
    st += [pltpu.make_async_copy(rq, q_o, loc.at[8]), pltpu.make_async_copy(dh, dh_o, loc.at[9])]
    for s in st[2:]:
        s.start()
    ones = jnp.ones((8, R), BF)

    def bd_step(n, carry):
        col = pl.ds(pl.multiple_of(n * 512, 512), 512)
        dbd_ref[:, col] = dot(ones, rq[:, col])[:1]
        return carry
    lax.fori_loop(0, D // 512, bd_step, 0)
    dbgu_ref[...] = dot(ones, dh[...])[:1]

    CW = 1024
    ln = lane((T, 128))

    def get_cols(base):
        pk = mcol[...]
        return [pk[:, base + k:base + k + 1] for k in range(4)]

    def hits(e):
        cd = get_cols(0)
        pos = (e * C + lane((T, C))).astype(F32)
        return [cd[k] == pos for k in range(4)]

    def ret_loop(buf, dst, ss, rs, first, body, carry):
        own = pltpu.make_async_copy(buf.at[pl.ds(pl.multiple_of(me * C, 16), C)], dst.at[me], loc.at[first])
        own.start()
        own.wait()

        def step(i, c):
            e = flip(me, i)

            @pl.when(i > 0)
            def _():
                remote(buf.at[pl.ds(0, C)], dst.at[e], ss.at[i], rs.at[i], e).wait_recv()
            get = pltpu.make_async_copy(dst.at[e], xs.at[0, pl.ds(0, C)], loc.at[first])
            get.start()
            get.wait()
            return body(e, c)
        return lax.fori_loop(0, NDEV, step, carry)

    acc[...] = jnp.zeros((T, D), F32)

    def add_y(e, rs):
        hk, gt = hits(e), get_cols(4)
        cw = jnp.zeros((T, C), F32)
        for k in range(4):
            cw = jnp.where(hk[k], gt[k], cw)
        c3 = jnp.concatenate(split3(cw), axis=0)
        for c in range(D // CW):
            cc = slice(c * CW, (c + 1) * CW)
            v = dot(c3, xs[0, :C, cc])
            acc[:, cc] += v[:T] + v[T:2 * T] + v[2 * T:]
        rm = dot_nt(dyv[...], xs[0, :C, :])
        return tuple(rs[k] + jnp.sum(jnp.where(hk[k], rm, 0.0), axis=1, keepdims=True) for k in range(4))

    zero = jnp.zeros((T, 1), F32)
    rk = ret_loop(yv, yret, ya_s, ya_r, 10, add_y, (zero,) * 4)
    gt, ei = get_cols(4), get_cols(8)
    mean = gt[0] * rk[0] + gt[1] * rk[1] + gt[2] * rk[2] + gt[3] * rk[3]
    dl = jnp.zeros((T, 128), F32)
    for k in range(4):
        dl = jnp.where(ei[k] == ln.astype(F32), gt[k] * (rk[k] - mean), dl)
    dlall[me] = dl.T[:NDEV].astype(BF)
    out_ref[...] = acc[...].astype(BF)
    dlb = dl.astype(BF)[:, :NDEV]

    def dl_copy(m):
        return remote(dlall.at[me], dlall.at[me], dl_s.at[m], dl_r.at[m], flip(me, m))

    for m in range(1, NDEV):
        dl_copy(m).start()
    for m in second:
        ret_copy(pv, pret, pa_s, pa_r, m).start()
    for c in range(D // CW):
        cc = slice(c * CW, (c + 1) * CW)
        acc[:, cc] = dot(dlb, wr_ref[:, cc])

    for m in range(1, NDEV):
        e = flip(me, m)
        remote(dlall.at[me], dlall.at[e], dl_s.at[m], dl_r.at[m], e).wait_recv()
    dwr_ref[...] = jnp.zeros(dwr_ref.shape, F32)

    def wr_begin(i):
        for j in range(3):
            load_part(0, j, flip(flip(me, i % 2), plane[j][i // 2]), i % 2).start()
    wr_begin(0)
    for i in range(8):
        if i < 7:
            wr_begin(i + 1)
        for j in range(3):
            s = flip(flip(me, i % 2), plane[j][i // 2])
            load_part(0, j, s, i % 2).wait()
            dwr_ref[:, cuts[j]:cuts[j + 1]] += dot(dlall[s], xs[i % 2, :, cuts[j]:cuts[j + 1]])

    def wr_copy(j):
        return remote(dwr_ref.at[:, cols(j)], wpart.at[:, cols(j)], wr_s.at[j], wr_r.at[j], flip(me, dims[j][2]))

    dbr = jnp.zeros((8, NDEV), F32)
    for s in range(NDEV):
        dbr = dbr + dot_nt(jnp.ones((8, T), BF), dlall[s])
    dbr_ref[...] = dbr[:1]
    for j in range(3):
        wr_copy(j).start()
    for m in last:
        ret_copy(pv, pret, pa_s, pa_r, m).start()

    def add_p(e, carry):
        hk = hits(e)
        hit = jnp.zeros((T, C), F32)
        for k in range(4):
            hit = jnp.where(hk[k], 1.0, hit)
        hb = hit.astype(BF)
        for c in range(D // CW):
            cc = slice(c * CW, (c + 1) * CW)
            acc[:, cc] += dot(hb, xs[0, :C, cc])
        return carry
    ret_loop(pv, pret, pa_s, pa_r, 11, add_p, 0)
    dx_ref[...] = acc[...].astype(BF)
    for j in range(3):
        wr_copy(j).wait()
    dwr_ref[...] = dwr_ref[...] + wpart[...]

    for w in range(2):
        for j in range(3):
            for idx in range(3):
                ag_copy(w, j, idx).wait_send()
            for t in range(4):
                co_copy(w, j, t).wait_send()
    for m in range(1, NDEV):
        meta_copy(m).wait_send()
        dl_copy(m).wait_send()
        ret_copy(yv, yret, ya_s, ya_r, m).wait_send()
        ret_copy(pv, pret, pa_s, pa_r, m).wait_send()
    for s in st:
        s.wait()


def solution(mesh):
    def local_block(hidden, grad_out, w_router, b_router, expert_ids, slot_ids, w_gate_up, b_gate_up, w_down, b_down):
        T, D = hidden.shape
        F = w_down.shape[1]
        C = (3 * T * 4 + 2 * NDEV - 1) // (2 * NDEV)
        R = NDEV * C
        NT = -(-F // 128)
        FP = NT * 128
        bias = jnp.pad(b_gate_up.reshape(F, 2), ((0, FP - F), (0, 0))).reshape(NT, 128, 2)
        bias = bias.transpose(0, 2, 1).reshape(NT, 1, 256)
        S = jax.ShapeDtypeStruct
        vm, hb = pl.BlockSpec(memory_space=pltpu.VMEM), pl.BlockSpec(memory_space=pl.ANY)
        outs = [S((T, D), BF), S((T, D), BF), S((NDEV, D), F32), S((1, NDEV), F32), S((1, D), F32), S((1, 2 * F), F32),
                S((R, D), BF), S((R, D), BF), S((R, FP), BF), S((R, 2 * F), BF),
                S((NDEV, T, D), BF), S((NDEV, T, D), BF), S((NDEV, C, D), BF), S((NDEV, C, D), BF)]
        V, dma = pltpu.VMEM, pltpu.SemaphoreType.DMA
        scratch = [V((2 * F, D), BF), V((FP, D), BF), V((R, D), BF), V((R, D), BF), V((R, FP), F32), V((R, FP), F32),
                   V((R, FP), BF), V((R, 2 * F), BF), V((R, D), BF), V((R, D), BF), V((2, T, D), BF), V((T, D), BF),
                   V((T, D), BF), V((T, D), F32), V((NDEV, 8, T), F32), V((NDEV, NDEV, T), BF), V((T, 128), F32),
                   V((256, 256), BF), V((NDEV, D), F32),
                   dma((2, 3, 3)), dma((2, 3, 3)), dma((2, 3, 4)), dma((2, 3, 4)), dma((2, 3, 4, 2)), dma((2, 3, 4, 2)),
                   dma((16,)), dma((16,)), dma((16,)), dma((16,)), dma((16,)), dma((16,)), dma((16,)), dma((16,)),
                   dma((3,)), dma((3,)), dma((12,)), dma((2, 3))]
        res = pl.pallas_call(
            functools.partial(block_kernel, (T, D, F, C)),
            out_shape=outs,
            in_specs=[hb, hb, vm, vm, vm, vm, hb, vm, hb, vm],
            out_specs=[vm, vm, vm, vm, vm, vm] + [hb] * 8,
            scratch_shapes=scratch,
            compiler_params=pltpu.CompilerParams(collective_id=0, has_side_effects=True, vmem_limit_bytes=67043328),
            name="moe_block",
        )(hidden, grad_out, w_router.T, b_router.reshape(NDEV, 1), expert_ids.T, slot_ids.T,
          w_gate_up[0].T, bias, w_down[0], b_down)
        out, dx, dwr, dbr, dbd, dbgu, rx, q, a, dh = res[:10]
        grad_w_down = jnp.einsum('rf,rd->fd', a[:, :F], q, preferred_element_type=F32)[None]
        grad_w_gate_up = jnp.einsum('rd,rf->df', rx, dh, preferred_element_type=F32)[None]
        return (out, dx, dwr.T, dbr[0], grad_w_gate_up, dbgu, grad_w_down, dbd)

    tok = P('ep', None)
    ex3, ex2 = P('ep', None, None), P('ep', None)
    in_specs = (tok, tok, P(None, None), P(None), tok, tok, ex3, ex2, ex3, ex2)
    out_specs = (tok, tok, P(None, None), P(None), ex3, ex2, ex3, ex2)
    return jax.shard_map(local_block, mesh=mesh, in_specs=in_specs, out_specs=out_specs, check_vma=False)
```

time: 363 us -> 296 us (0.82); the launches traced: 361 us -> 291 us
  Pallas kernels: 307 us -> 258 us
  local copies, waits for them, and re-layouts: 26.9 us -> 6.79 us
    pallas_call x1, Pallas kernels: 307 us -> 258 us  [local_block(): pl.pallas_call(functools.partial(block_kernel, (T, D, F, C)), out_shape=o...]
    unnamed x17 -> x22, local copies, waits for them, and re-layouts: 23 us -> 4.39 us
where the time goes in v2:
time: 296 us; the launch traced here: 291 us
  Pallas kernels  258 us (87%)
  matrix products  24.5 us (8%)
  local copies, waits for them, and re-layouts  6.79 us (2%)
    pallas_call x1, Pallas kernels, local_block(): pl.pallas_call(functools.partial(block_kernel, (T, D, F, C)), out_shape=o...  258 us
    dot_general x1, matrix products, local_block(): jnp.einsum('rf,rd->fd', a[:, :F], q, preferred_element_type=F32)[None]  12.2 us
    dot_general x1, matrix products, local_block(): jnp.einsum('rd,rf->df', rx, dh, preferred_element_type=F32)[None]  12.2 us

profile of v2, /device:TPU:0, one launch (start us, length us, event | category | flops | bytes accessed | tf_op | source)
XLA Modules:
  0.0 290.5 jit_solution(9426966996828743403)
XLA Ops:
  0.6 1.3 copy.21.refs_3_
  2.0 0.7 reduce
  2.7 0.3 reshape.29
  3.0 0.7 copy.20
  3.8 257.8 %moe_block.1 = (bf16[128,4096]{1,0:T(8,128)(2,1)}, bf16[128,4096]{1,0:T(8,128)(2,1)}, f32[16,4096]{1,0:T(8,128)}, f32[1,16]{1,0:T(1,128)}, f32[1,4096]{1,0:T(1,1...) custom-call(bf16[128,4096]{1,0:T(8,128)(2,1)} %refs_0_.1, ...), custom_call_target="tpu_custom_call" | custom-call | tf_op jit(solution)/shard_map/moe_block/pallas_call | solution.py:517
  261.6 0.0 copy-start.5
  261.6 0.0 copy-start.6
  261.6 12.2 %convolution_bitcast_fusion.1 = f32[1,688,4096]{2,1,0:T(8,128)} fusion(bf16[768,4096]{1,0:T(8,128)(2,1)} %get-tuple-element.26, bf16[768,768]{1,0:T(8,128)(2,1)} %get-tuple-element.25), kind=kOutput, calls=%fused_computation.1 | convolution fusion | flops 4328521728 | bytes 18743296 | tf_op jit(solution)/shard_map/rf,rd->fd/dot_general | solution.py:528
  273.9 0.0 copy-done.5
  273.9 0.0 copy-done.6
  273.9 0.0 copy-start.1
  273.9 0.0 copy-start
  273.9 0.0 copy-start.2
  273.9 0.0 copy-start.7
  273.9 0.0 copy-start.4
  273.9 0.0 copy-start.3
  273.9 12.2 %convolution_bitcast_fusion = f32[1,4096,1376]{1,2,0:T(8,128)} fusion(bf16[768,4096]{1,0:T(8,128)(2,1)S(1)} %copy-done.5, bf16[768,1376]{1,0:T(8,128)(2,1)S(1)} %copy-done.6), kind=kOutput, calls=%fused_computation | convolution fusion | flops 8657043456 | bytes 30949376 | tf_op jit(solution)/shard_map/rd,rf->df/dot_general | solution.py:529
  286.1 0.0 copy-done.1
  286.1 1.0 copy.30
  287.1 0.0 copy-done
  287.1 1.0 copy.31
  288.1 0.0 copy-done.2
  288.1 0.7 copy.32
  288.8 0.0 copy-done.7
  288.8 0.5 copy.33
  289.3 0.0 copy-done.4
  289.3 0.6 copy.34
  289.9 0.0 copy-done.3
  289.9 0.6 copy.35
  (1 shorter events, 0.0 us)
Async XLA Ops:
  261.6 12.3 %copy-start.5 = (bf16[768,4096]{1,0:T(8,128)(2,1)S(1)}, bf16[768,4096]{1,0:T(8,128)(2,1)}, u32[]{:S(2)}) copy-start(bf16[768,4096]{1,0:T(8,128)(2,1)} %get-tuple-element.22) | copy-start | bytes 18874372
  261.6 12.3 %copy-start.6 = (bf16[768,1376]{1,0:T(8,128)(2,1)S(1)}, bf16[768,1376]{1,0:T(8,128)(2,1)}, u32[]{:S(2)}) copy-start(bf16[768,1376]{1,0:T(8,128)(2,1)} %get-tuple-element.23) | copy-start | bytes 6340612
  273.9 12.3 %copy-start.1 = (bf16[128,4096]{1,0:T(8,128)(2,1)S(1)}, bf16[128,4096]{1,0:T(8,128)(2,1)}, u32[]{:S(2)}) copy-start(bf16[128,4096]{1,0:T(8,128)(2,1)} %get-tuple-element.36) | copy-start | bytes 3145732
  273.9 13.3 %copy-start = (bf16[128,4096]{1,0:T(8,128)(2,1)S(1)}, bf16[128,4096]{1,0:T(8,128)(2,1)}, u32[]{:S(2)}) copy-start(bf16[128,4096]{1,0:T(8,128)(2,1)} %get-tuple-element.37) | copy-start | bytes 3145732
  273.9 14.2 %copy-start.2 = (f32[16,4096]{1,0:T(8,128)S(1)}, f32[16,4096]{1,0:T(8,128)}, u32[]{:S(2)}) copy-start(f32[16,4096]{1,0:T(8,128)} %get-tuple-element.20) | copy-start | bytes 786436
  273.9 14.9 %copy-start.7 = (f32[1,16]{1,0:T(1,128)S(1)}, f32[1,16]{1,0:T(1,128)}, u32[]{:S(2)}) copy-start(f32[1,16]{1,0:T(1,128)} %get-tuple-element.21) | copy-start | bytes 196
  273.9 15.4 %copy-start.4 = (f32[1,1376]{1,0:T(1,128)S(1)}, f32[1,1376]{1,0:T(1,128)}, u32[]{:S(2)}) copy-start(f32[1,1376]{1,0:T(1,128)} %get-tuple-element.41) | copy-start | bytes 16516
  273.9 16.0 %copy-start.3 = (f32[1,4096]{1,0:T(1,128)S(1)}, f32[1,4096]{1,0:T(1,128)}, u32[]{:S(2)}) copy-start(f32[1,4096]{1,0:T(1,128)} %get-tuple-element.43) | copy-start | bytes 49156
